TPU v7x, 16 devices: a 4x2x1 block of a 4x4x8 slice. The times are simulated.
16 devices in a mesh: rep: 2 (over y, z), data: 8 (over x, core).
Axes of the slice: x: 4, y: 2, z: 1, core: 2. Of those that a mesh axis runs over, the one named last changes fastest.
The devices are a block of a 4x4x8 slice.
Arguments:
- x: bfloat16 [1024, 1536], P(('rep', 'data')), parts along dimension 0
- adapter_id: int32 [1024], P(('rep', 'data')), parts along dimension 0
- w_gate: bfloat16 [1536, 8960], replicated
- w_up: bfloat16 [1536, 8960], replicated
- w_down: bfloat16 [8960, 1536], replicated
- a_gate: bfloat16 [1024, 8, 1536], P('data')
- b_gate: bfloat16 [1024, 8, 8960], P('data')
- a_up: bfloat16 [1024, 8, 1536], P('data')
- b_up: bfloat16 [1024, 8, 8960], P('data')
- a_down: bfloat16 [1024, 8, 8960], P('data')
- b_down: bfloat16 [1024, 8, 1536], P('data')
Outputs:
- output: bfloat16 [1024, 1536], P(('rep', 'data')), parts along dimension 0
There are 2 independent parts. A program takes and returns all parts, laid end to end along the dimension named above; an argument that names none is the same for every part.
All inputs are finite; a program needn't handle non-finite values.
Results may differ from a plain program's by a relative error of at most 0.00571002.
Values are sent between devices in bfloat16 or wider.
A program may use at most 768 MiB of HBM per device.

v0:
```python
import jax
import jax.numpy as jnp
from jax import lax
from jax.sharding import PartitionSpec as P, NamedSharding

value_a10 = 32


def value_a9(tok_rows, row_ids, a_mat, b_mat):
    array_b10 = value_a10 / a_mat.shape[1]
    a_rows = jnp.take(a_mat, row_ids, axis=0)
    b_rows = jnp.take(b_mat, row_ids, axis=0)
    low_rank = jnp.einsum("md,mrd->mr", tok_rows, a_rows, preferred_element_type=jnp.float32).astype(jnp.bfloat16)
    full_rows = jnp.einsum("ns,nsg->ng", low_rank, b_rows, preferred_element_type=jnp.float32)
    return (array_b10 * full_rows).astype(jnp.bfloat16)


def solution(mesh):
    groups = mesh.shape["data"]
    row_spec = P(("rep", "data"), None)
    id_spec = P(("rep", "data"))
    owned_spec = P("data", None, None)

    def device_step(x, adapter_id, w_gate, w_up, w_down, a_gate, b_gate, a_up, b_up, a_down, b_down):
        tok_count = x.shape[0]
        per_owner = a_gate.shape[0]
        capacity = (3 * tok_count + groups - 1) // groups
        owner_idx = adapter_id // per_owner
        local_ad = adapter_id % per_owner
        owner_hot = (owner_idx[:, None] == jnp.arange(groups)[None, :]).astype(jnp.int32)
        arrival = jnp.sum(jnp.cumsum(owner_hot, axis=0) * owner_hot, axis=1) - 1
        slot_idx = owner_idx * capacity + arrival
        slot_hot = (slot_idx[:, None] == jnp.arange(groups * capacity)[None, :]).astype(jnp.int32)
        dispatch = slot_hot.astype(jnp.bfloat16)
        send_ids = jnp.sum(slot_hot * local_ad[:, None], axis=0)
        send_x = jnp.einsum("tm,td->md", dispatch, x, preferred_element_type=jnp.float32).astype(jnp.bfloat16)
        recv_ids = lax.all_to_all(send_ids, "data", 0, 0, tiled=True)
        recv_x = lax.all_to_all(send_x, "data", 0, 0, tiled=True)
        gate_back = lax.all_to_all(value_a9(recv_x, recv_ids, a_gate, b_gate), "data", 0, 0, tiled=True)
        up_back = lax.all_to_all(value_a9(recv_x, recv_ids, a_up, b_up), "data", 0, 0, tiled=True)
        gate_pre = jnp.dot(x, w_gate, preferred_element_type=jnp.float32) + jnp.einsum("tm,mf->tf", dispatch, gate_back, preferred_element_type=jnp.float32)
        up_pre = jnp.dot(x, w_up, preferred_element_type=jnp.float32) + jnp.einsum("tm,mf->tf", dispatch, up_back, preferred_element_type=jnp.float32)
        hidden = (jax.nn.silu(gate_pre) * up_pre).astype(jnp.bfloat16)
        send_h = jnp.einsum("tm,tf->mf", dispatch, hidden, preferred_element_type=jnp.float32).astype(jnp.bfloat16)
        recv_h = lax.all_to_all(send_h, "data", 0, 0, tiled=True)
        down_back = lax.all_to_all(value_a9(recv_h, recv_ids, a_down, b_down), "data", 0, 0, tiled=True)
        down_out = jnp.dot(hidden, w_down, preferred_element_type=jnp.float32) + jnp.einsum("tm,md->td", dispatch, down_back, preferred_element_type=jnp.float32)
        return (x.astype(jnp.float32) + down_out).astype(jnp.bfloat16)

    return jax.shard_map(device_step, mesh=mesh, in_specs=(row_spec, id_spec, P(), P(), P(), owned_spec, owned_spec, owned_spec, owned_spec, owned_spec, owned_spec), out_specs=row_spec, check_vma=False)
```

profile of v0, /device:TPU:113, one launch (start us, length us, event | category | flops | bytes accessed | tf_op | source)
XLA Modules:
  0.0 275.1 jit_solution(14924440954119652474)
XLA Ops:
  2.0 6.0 %all-to-all-start.1 = ((s32[8,24,1]{1,2,0:T(1,128)}), s32[8,24,1]{1,2,0:T(1,128)S(1)}, u32[]{:S(2)}, u32[]{:S(2)}) async-start(s32[8,24,1]{1,2,0:T(1,128)} %bitcast.3), calls=%async_computation.1 | async-start | bytes 8192 | tf_op jit(solution)/shard_map/all_to_all | solution.py:37
  12.4 4.8 %all-to-all-start = ((bf16[8,24,1536]{2,1,0:T(8,128)(2,1)}), bf16[8,24,1536]{2,1,0:T(8,128)(2,1)}, u32[]{:S(2)}, u32[]{:S(2)}) async-start(bf16[8,24,1536]{2,1,0:T(8,128)(2,1)} %bitcast.54), calls=%async_computation | async-start | bytes 1179648 | tf_op jit(solution)/shard_map/all_to_all | solution.py:38
  18.5 3.4 %gather_fusion = bf16[192,8,1536]{2,1,0:T(8,128)(2,1)} fusion(bf16[128,8,1536]{2,1,0:T(8,128)(2,1)S(1)} %copy-done, s32[1024]{0:T(1024)S(1)} %pad_clamp_fusion), kind=kCustom, calls=%fused_computation.clone | custom fusion | bytes 9437952 | tf_op jit(solution)/shard_map/jit(_take)/gather | solution.py:11
  21.9 18.4 %gather_fusion.1 = bf16[192,8,8960]{2,1,0:T(8,128)(2,1)} fusion(bf16[128,8,8960]{2,1,0:T(8,128)(2,1)} %param.21, s32[1024]{0:T(1024)S(1)} %pad_clamp_fusion), kind=kCustom, calls=%fused_computation.1.clone | custom fusion | bytes 55051008 | tf_op jit(solution)/shard_map/jit(_take)/gather | solution.py:12
  43.6 18.4 %gather_fusion.3 = bf16[192,8,8960]{2,1,0:T(8,128)(2,1)} fusion(bf16[128,8,8960]{2,1,0:T(8,128)(2,1)} %param.23, s32[1024]{0:T(1024)S(1)} %pad_clamp_fusion), kind=kCustom, calls=%fused_computation.4.clone | custom fusion | bytes 55051008 | tf_op jit(solution)/shard_map/jit(_take)/gather | solution.py:12
  62.0 6.0 %fusion.21 = f32[192,1,8]{2,1,0:T(1,128)S(1)} fusion(bf16[192,8,1536]{2,1,0:T(8,128)(2,1)} %gather_fusion, pred[192]{0:T(512)(128)(4,1)S(1)} %compare_and_fusion, bf16[192,1536,1]{1,0,2:T(8,128)(2,1)} %bitcast.2), kind=kOutput, calls=%fused_computation.32 | convolution fusion | flops 7077888 | bytes 5314752 | tf_op jit(solution)/shard_map/md,mrd->mr/dot_general | solution.py:13
  68.0 12.2 %fusion.4 = f32[192,1,8960]{2,1,0:T(1,128)S(1)} fusion(bf16[192,8,8960]{2,1,0:T(8,128)(2,1)} %gather_fusion.1, pred[192]{0:T(512)(128)(4,1)S(1)} %compare_and_fusion, bf16[192,8,1]{1,0,2:T(8,128)(2,1)S(1)} %convert_bitcast_fusion.2), kind=kOutput, calls=%fused_computation.10 | convolution fusion | flops 41287680 | bytes 34409664 | tf_op jit(solution)/shard_map/ns,nsg->ng/dot_general | solution.py:14
  82.5 4.7 %all-to-all-start.2 = ((bf16[8,24,8960]{2,1,0:T(8,128)(2,1)}), bf16[8,24,8960]{2,1,0:T(8,128)(2,1)}, u32[]{:S(2)}, u32[]{:S(2)}) async-start(bf16[8,24,8960]{2,1,0:T(8,128)(2,1)} %bitcast.51), calls=%async_computation.2 | async-start | bytes 6881280 | tf_op jit(solution)/shard_map/all_to_all | solution.py:39
  87.2 6.0 %fusion.19 = f32[192,1,8]{2,1,0:T(1,128)S(1)} fusion(bf16[192,8,1536]{2,1,0:T(8,128)(2,1)} %gather_fusion.2, pred[192]{0:T(512)(128)(4,1)S(1)} %compare_and_fusion, bf16[192,1536,1]{1,0,2:T(8,128)(2,1)} %bitcast.2), kind=kOutput, calls=%fused_computation.30 | convolution fusion | flops 7077888 | bytes 5314752 | tf_op jit(solution)/shard_map/md,mrd->mr/dot_general | solution.py:13
  93.3 12.2 %fusion.2 = f32[192,1,8960]{2,1,0:T(1,128)S(1)} fusion(bf16[192,8,8960]{2,1,0:T(8,128)(2,1)} %gather_fusion.3, pred[192]{0:T(512)(128)(4,1)S(1)} %compare_and_fusion, bf16[192,8,1]{1,0,2:T(8,128)(2,1)S(1)} %convert_bitcast_fusion.1), kind=kOutput, calls=%fused_computation.8 | convolution fusion | flops 41287680 | bytes 34409664 | tf_op jit(solution)/shard_map/ns,nsg->ng/dot_general | solution.py:14
  107.7 18.9 %all-to-all-done.2 = bf16[8,24,8960]{2,1,0:T(8,128)(2,1)} async-done(((bf16[8,24,8960]{2,1,0:T(8,128)(2,1)}), bf16[8,24,8960]{2,1,0:T(8,128)(2,1)}, u32[]{:S(2)}, u32[]{:S(2)}) %all-to-all-start.2) | async-done | bytes 3440672 | tf_op jit(solution)/shard_map/all_to_all | solution.py:39
  126.7 5.4 %all-to-all-start.3 = ((bf16[8,24,8960]{2,1,0:T(8,128)(2,1)}), bf16[8,24,8960]{2,1,0:T(8,128)(2,1)}, u32[]{:S(2)}, u32[]{:S(2)}) async-start(bf16[8,24,8960]{2,1,0:T(8,128)(2,1)} %bitcast.52), calls=%async_computation.3 | async-start | bytes 6881280 | tf_op jit(solution)/shard_map/all_to_all | solution.py:40
  132.1 11.3 %fusion.49 = f32[64,8960]{1,0:T(8,128)S(1)} fusion(bf16[64,1536]{1,0:T(8,128)(2,1)S(1)} %copy-done.6, bf16[1536,8960]{1,0:T(8,128)(2,1)} %param.17), kind=kOutput, calls=%fused_computation.80 | convolution fusion | flops 1761607680 | bytes 30015488 | tf_op jit(solution)/shard_map/dot_general | solution.py:41
  143.4 12.8 %fusion.50 = f32[64,8960]{1,0:T(8,128)} fusion(bf16[64,1536]{1,0:T(8,128)(2,1)S(1)} %copy-done.6, bf16[1536,8960]{1,0:T(8,128)(2,1)} %param.18), kind=kOutput, calls=%fused_computation.81 | convolution fusion | flops 1761607680 | bytes 30015488 | tf_op jit(solution)/shard_map/dot_general | solution.py:42
  156.3 4.2 %convolution_add_fusion.1 = f32[64,8960]{1,0:T(8,128)} fusion(f32[64,8960]{1,0:T(8,128)S(1)} %fusion.49, bf16[192,8960]{1,0:T(8,128)(2,1)} %bitcast.9, s32[64]{0:T(128)S(1)} %add_add_fusion), kind=kOutput, calls=%fused_computation.21 | convolution fusion | flops 220811264 | bytes 8028416 | tf_op jit(solution)/shard_map/tm,mf->tf/dot_general | solution.py:41
  160.4 12.3 %all-to-all-done.3 = bf16[8,24,8960]{2,1,0:T(8,128)(2,1)} async-done(((bf16[8,24,8960]{2,1,0:T(8,128)(2,1)}), bf16[8,24,8960]{2,1,0:T(8,128)(2,1)}, u32[]{:S(2)}, u32[]{:S(2)}) %all-to-all-start.3) | async-done | bytes 3440672 | tf_op jit(solution)/shard_map/all_to_all | solution.py:40
  172.7 4.4 %fusion.13 = bf16[64,8960]{1,0:T(8,128)(2,1)S(1)} fusion(f32[64,8960]{1,0:T(8,128)} %fusion.50, bf16[192,8960]{1,0:T(8,128)(2,1)} %bitcast.15, f32[64,8960]{1,0:T(8,128)} %convolution_add_fusion.1, s32[64]{0:T(128)S(1)} %add_add_fusion), kind=kOutput, calls=%fused_computation.22 | convolution fusion | flops 224251904 | bytes 9175296 | tf_op jit(solution)/shard_map/tm,mf->tf/dot_general | solution.py:42
  180.0 5.5 %all-to-all-start.4 = ((bf16[8,24,8960]{2,1,0:T(8,128)(2,1)}), bf16[8,24,8960]{2,1,0:T(8,128)(2,1)}, u32[]{:S(2)}, u32[]{:S(2)}) async-start(bf16[8,24,8960]{2,1,0:T(8,128)(2,1)} %bitcast.53), calls=%async_computation.4 | async-start | bytes 6881280 | tf_op jit(solution)/shard_map/all_to_all | solution.py:45
  185.5 18.6 %gather_fusion.4 = bf16[192,8,8960]{2,1,0:T(8,128)(2,1)} fusion(bf16[128,8,8960]{2,1,0:T(8,128)(2,1)} %param.24, s32[1024]{0:T(1024)S(1)} %pad_clamp_fusion), kind=kCustom, calls=%fused_computation.5.clone | custom fusion | bytes 55051008 | tf_op jit(solution)/shard_map/jit(_take)/gather | solution.py:11
  204.1 3.4 %gather_fusion.5 = bf16[192,8,1536]{2,1,0:T(8,128)(2,1)} fusion(bf16[128,8,1536]{2,1,0:T(8,128)(2,1)S(1)} %copy-done.3, s32[1024]{0:T(1024)S(1)} %pad_clamp_fusion), kind=kCustom, calls=%fused_computation.3.clone | custom fusion | bytes 9437952 | tf_op jit(solution)/shard_map/jit(_take)/gather | solution.py:12
  207.4 18.6 %all-to-all-done.4 = bf16[8,24,8960]{2,1,0:T(8,128)(2,1)} async-done(((bf16[8,24,8960]{2,1,0:T(8,128)(2,1)}), bf16[8,24,8960]{2,1,0:T(8,128)(2,1)}, u32[]{:S(2)}, u32[]{:S(2)}) %all-to-all-start.4) | async-done | bytes 3440672 | tf_op jit(solution)/shard_map/all_to_all | solution.py:45
  226.1 23.8 %fusion = f32[192,1,8]{2,1,0:T(1,128)S(1)} fusion(bf16[192,8,8960]{2,1,0:T(8,128)(2,1)} %gather_fusion.4, pred[192]{0:T(512)(128)(4,1)S(1)} %compare_and_fusion, bf16[192,8960,1]{1,0,2:T(8,128)(2,1)} %bitcast.18), kind=kOutput, calls=%fused_computation.6 | convolution fusion | flops 41287680 | bytes 30972096 | tf_op jit(solution)/shard_map/md,mrd->mr/dot_general | solution.py:13
  252.8 5.2 %all-to-all-start.5 = ((bf16[8,24,1536]{2,1,0:T(8,128)(2,1)}), bf16[8,24,1536]{2,1,0:T(8,128)(2,1)}, u32[]{:S(2)}, u32[]{:S(2)}) async-start(bf16[8,24,1536]{2,1,0:T(8,128)(2,1)} %bitcast.23), calls=%async_computation.5 | async-start | bytes 1179648 | tf_op jit(solution)/shard_map/all_to_all | solution.py:46
  258.0 14.9 %fusion.51 = f32[64,1536]{1,0:T(8,128)} fusion(bf16[64,8960]{1,0:T(8,128)(2,1)} %copy-done.4, bf16[8960,1536]{1,0:T(8,128)(2,1)} %param.19), kind=kOutput, calls=%fused_computation.82 | convolution fusion | flops 1761607680 | bytes 29065216 | tf_op jit(solution)/shard_map/dot_general | solution.py:47
  (41 shorter events, 23.4 us)
Async XLA Ops:
  0.0 18.5 %copy-start = (bf16[128,8,1536]{2,1,0:T(8,128)(2,1)S(1)}, bf16[128,8,1536]{2,1,0:T(8,128)(2,1)}, u32[]{:S(2)}) copy-start(bf16[128,8,1536]{2,1,0:T(8,128)(2,1)} %param.20) | copy-start | bytes 9437188
  2.0 10.4 %all-to-all-start.1 = ((s32[8,24,1]{1,2,0:T(1,128)}), s32[8,24,1]{1,2,0:T(1,128)S(1)}, u32[]{:S(2)}, u32[]{:S(2)}) async-start(s32[8,24,1]{1,2,0:T(1,128)} %bitcast.3), calls=%async_computation.1 | async-start | bytes 8192 | tf_op jit(solution)/shard_map/all_to_all | solution.py:37
  12.4 49.6 %all-to-all-start = ((bf16[8,24,1536]{2,1,0:T(8,128)(2,1)}), bf16[8,24,1536]{2,1,0:T(8,128)(2,1)}, u32[]{:S(2)}, u32[]{:S(2)}) async-start(bf16[8,24,1536]{2,1,0:T(8,128)(2,1)} %bitcast.54), calls=%async_computation | async-start | bytes 1179648 | tf_op jit(solution)/shard_map/all_to_all | solution.py:38
  21.9 18.4 %copy-start.2 = (bf16[128,8,1536]{2,1,0:T(8,128)(2,1)S(1)}, bf16[128,8,1536]{2,1,0:T(8,128)(2,1)}, u32[]{:S(2)}) copy-start(bf16[128,8,1536]{2,1,0:T(8,128)(2,1)} %param.22) | copy-start | bytes 9437188
  82.5 44.2 %all-to-all-start.2 = ((bf16[8,24,8960]{2,1,0:T(8,128)(2,1)}), bf16[8,24,8960]{2,1,0:T(8,128)(2,1)}, u32[]{:S(2)}, u32[]{:S(2)}) async-start(bf16[8,24,8960]{2,1,0:T(8,128)(2,1)} %bitcast.51), calls=%async_computation.2 | async-start | bytes 6881280 | tf_op jit(solution)/shard_map/all_to_all | solution.py:39
  107.7 24.4 %copy-start.6 = (bf16[64,1536]{1,0:T(8,128)(2,1)S(1)}, bf16[64,1536]{1,0:T(8,128)(2,1)}, u32[]{:S(2)}) copy-start(bf16[64,1536]{1,0:T(8,128)(2,1)} %param.15) | copy-start | bytes 589828
  126.7 46.0 %all-to-all-start.3 = ((bf16[8,24,8960]{2,1,0:T(8,128)(2,1)}), bf16[8,24,8960]{2,1,0:T(8,128)(2,1)}, u32[]{:S(2)}, u32[]{:S(2)}) async-start(bf16[8,24,8960]{2,1,0:T(8,128)(2,1)} %bitcast.52), calls=%async_computation.3 | async-start | bytes 6881280 | tf_op jit(solution)/shard_map/all_to_all | solution.py:40
  177.1 2.9 %copy-start.4 = (bf16[64,8960]{1,0:T(8,128)(2,1)}, bf16[64,8960]{1,0:T(8,128)(2,1)S(1)}, u32[]{:S(2)}) copy-start(bf16[64,8960]{1,0:T(8,128)(2,1)S(1)} %fusion.13) | copy-start | bytes 3440644
  180.0 46.1 %all-to-all-start.4 = ((bf16[8,24,8960]{2,1,0:T(8,128)(2,1)}), bf16[8,24,8960]{2,1,0:T(8,128)(2,1)}, u32[]{:S(2)}, u32[]{:S(2)}) async-start(bf16[8,24,8960]{2,1,0:T(8,128)(2,1)} %bitcast.53), calls=%async_computation.4 | async-start | bytes 6881280 | tf_op jit(solution)/shard_map/all_to_all | solution.py:45
  185.5 18.6 %copy-start.3 = (bf16[128,8,1536]{2,1,0:T(8,128)(2,1)S(1)}, bf16[128,8,1536]{2,1,0:T(8,128)(2,1)}, u32[]{:S(2)}) copy-start(bf16[128,8,1536]{2,1,0:T(8,128)(2,1)} %param.25) | copy-start | bytes 9437188
  226.1 23.9 %copy-start.5 = (bf16[192,8,1536]{2,1,0:T(8,128)(2,1)S(1)}, bf16[192,8,1536]{2,1,0:T(8,128)(2,1)}, u32[]{:S(2)}) copy-start(bf16[192,8,1536]{2,1,0:T(8,128)(2,1)} %gather_fusion.5) | copy-start | bytes 14155780
  252.8 20.1 %all-to-all-start.5 = ((bf16[8,24,1536]{2,1,0:T(8,128)(2,1)}), bf16[8,24,1536]{2,1,0:T(8,128)(2,1)}, u32[]{:S(2)}, u32[]{:S(2)}) async-start(bf16[8,24,1536]{2,1,0:T(8,128)(2,1)} %bitcast.23), calls=%async_computation.5 | async-start | bytes 1179648 | tf_op jit(solution)/shard_map/all_to_all | solution.py:46
  258.0 17.1 %copy-start.1 = (bf16[128,8,1536]{2,1,0:T(8,128)(2,1)S(1)}, bf16[128,8,1536]{2,1,0:T(8,128)(2,1)}, u32[]{:S(2)}) copy-start(bf16[128,8,1536]{2,1,0:T(8,128)(2,1)} %param.20) | copy-start | bytes 9437188
where the time goes:
time: 277 us; the launch traced here: 275 us
  matrix products  117 us (42%)
  local copies, waits for them, and re-layouts  66.8 us (24%)
  waiting for transfers between devices  52.1 us (19%)
  starting transfers between devices  31.6 us (11%)
  other arithmetic  7.41 us (3%)
    gather x3, local copies, waits for them, and re-layouts, value_a9(): b_rows = jnp.take(b_mat, row_ids, axis=0)  40.2 us
    dot_general x3, matrix products, value_a9(): jnp.einsum('md,mrd->mr', tok_rows, a_rows, preferred_element_type=jnp.flo...  35.8 us
    dot_general x3, matrix products, value_a9(): jnp.einsum('ns,nsg->ng', low_rank, b_rows, preferred_element_type=jnp.flo...  26.4 us
    gather x3, local copies, waits for them, and re-layouts, value_a9(): a_rows = jnp.take(a_mat, row_ids, axis=0)  25.2 us
    all_to_all x1, waiting for transfers between devices, device_step(): lax.all_to_all(value_a9(recv_x, recv_ids, a_gate, b_gate), 'data', 0, 0,...  18.9 us
    all_to_all x1, waiting for transfers between devices, device_step(): recv_h = lax.all_to_all(send_h, 'data', 0, 0, tiled=True)  18.6 us
    dot_general x1, matrix products, device_step(): jnp.dot(hidden, w_down, preferred_element_type=jnp.float32)  14.9 us
    dot_general x1, matrix products, device_step(): jnp.dot(x, w_up, preferred_element_type=jnp.float32)  12.8 us
  transfers between devices with their start and end apart: 6, of which 4 were waited for; matrix products, arithmetic and copies ran while one was open for 48% of the time, Pallas kernels for 0%

commit v1 on v0

v1 whole, which is shorter than its diff:
```python
import jax
import jax.numpy as jnp
from jax import lax
from jax.sharding import PartitionSpec as P

ALPHA = 32


def solution(mesh):
    groups = mesh.shape["data"]
    row_spec = P(("rep", "data"), None)
    id_spec = P(("rep", "data"))
    owned_spec = P("data", None, None)

    def device_step(x, adapter_id, w_gate, w_up, w_down, a_gate, b_gate, a_up, b_up, a_down, b_down):
        tok_count = x.shape[0]
        per_owner, rank, _ = a_gate.shape
        scale = ALPHA / rank
        capacity = (3 * tok_count + groups - 1) // groups
        owner_idx = adapter_id // per_owner
        local_ad = adapter_id % per_owner
        same = (owner_idx[:, None] == owner_idx[None, :]) & (jnp.arange(tok_count)[None, :] < jnp.arange(tok_count)[:, None])
        arrival = jnp.sum(same.astype(jnp.int32), axis=1)
        slot_idx = owner_idx * capacity + arrival
        dispatch = (slot_idx[:, None] == jnp.arange(groups * capacity)[None, :]).astype(jnp.bfloat16)
        id_cols = jnp.broadcast_to(local_ad.astype(jnp.bfloat16)[:, None], (tok_count, 128))
        payload = jnp.concatenate([x, id_cols], axis=1)
        send = jnp.einsum("tm,td->md", dispatch, payload, preferred_element_type=jnp.float32).astype(jnp.bfloat16)
        recv = lax.all_to_all(send, "data", 0, 0, tiled=True)
        rows = recv[:, : x.shape[1]]
        ids = recv[:, x.shape[1] : x.shape[1] + 1].astype(jnp.int32)
        own = ids == (jnp.arange(per_owner * rank) // rank)[None, :]

        def delta(v, a_mat, b_mat):
            low = lax.dot_general(v, a_mat.reshape(per_owner * rank, -1), (((1,), (1,)), ((), ())), preferred_element_type=jnp.float32)
            low = jnp.where(own, low, 0.0).astype(jnp.bfloat16)
            full = jnp.dot(low, b_mat.reshape(per_owner * rank, -1), preferred_element_type=jnp.float32)
            return (scale * full).astype(jnp.bfloat16).astype(jnp.float32)

        gate_pre = jnp.dot(rows, w_gate, preferred_element_type=jnp.float32) + delta(rows, a_gate, b_gate)
        up_pre = jnp.dot(rows, w_up, preferred_element_type=jnp.float32) + delta(rows, a_up, b_up)
        hidden = (jax.nn.silu(gate_pre) * up_pre).astype(jnp.bfloat16)
        down = jnp.dot(hidden, w_down, preferred_element_type=jnp.float32) + delta(hidden, a_down, b_down)
        done = (rows.astype(jnp.float32) + down).astype(jnp.bfloat16)
        back = lax.all_to_all(done, "data", 0, 0, tiled=True)
        return jnp.einsum("tm,md->td", dispatch, back, preferred_element_type=jnp.float32).astype(jnp.bfloat16)

    return jax.shard_map(device_step, mesh=mesh, in_specs=(row_spec, id_spec, P(), P(), P(), owned_spec, owned_spec, owned_spec, owned_spec, owned_spec, owned_spec), out_specs=row_spec, check_vma=False)
```

time: 277 us -> 123 us (0.44)
  local copies, waits for them, and re-layouts: 66.8 us -> 0.09 us
  waiting for transfers between devices: 52.1 us -> 10.5 us
  matrix products: 117 us -> 90.5 us
  starting transfers between devices: 31.6 us -> 6.02 us
  blocking collectives: 0 us -> 13.8 us
  other arithmetic: 7.41 us -> 1.91 us
    gather x6 -> x0, local copies, waits for them, and re-layouts: 65.5 us -> none  [the longest x3 40.2 us: value_a9(): b_rows = jnp.take(b_mat, row_ids, axis=0)]
    all_to_all x6 -> x1, waiting for transfers between devices: 52.1 us -> 10.5 us  [device_step(): recv = lax.all_to_all(send, 'data', 0, 0, tiled=True)]
    all_to_all x6 -> x1, starting transfers between devices: 31.6 us -> 6.02 us  [device_step(): recv = lax.all_to_all(send, 'data', 0, 0, tiled=True)]
    dot_general x13 -> x7, matrix products: 102 us -> 77.3 us  [the longest x3 39.3 us: delta(): jnp.dot(low, b_mat.reshape(per_owner * rank, -1), preferred_element_type=...]
    all_to_all x0 -> x1, blocking collectives: none -> 13.8 us  [device_step(): back = lax.all_to_all(done, 'data', 0, 0, tiled=True)]
    convert_element_type x7 -> x0, other arithmetic: 5.53 us -> none  [the longest x3 5.41 us: value_a9(): return (array_b10 * full_rows).astype(jnp.bfloat16)]
  transfers between devices with their start and end apart: 6 -> 1, of which waited for: 4 -> 1; matrix products, arithmetic and copies ran while one was open for 48% -> 0% of each run, Pallas kernels for 0% -> 0%
where the time goes in v1:
time: 123 us
  matrix products  90.5 us (74%)
  blocking collectives  13.8 us (11%)
  waiting for transfers between devices  10.5 us (9%)
  starting transfers between devices  6.02 us (5%)
  other arithmetic  1.91 us (2%)
    dot_general x3, matrix products, delta(): jnp.dot(low, b_mat.reshape(per_owner * rank, -1), preferred_element_type=...  39.3 us
    dot_general x1, matrix products, device_step(): jnp.dot(rows, w_up, preferred_element_type=jnp.float32)  18 us
    dot_general x1, matrix products, device_step(): jnp.dot(rows, w_gate, preferred_element_type=jnp.float32)  16.9 us
    all_to_all x1, blocking collectives, device_step(): back = lax.all_to_all(done, 'data', 0, 0, tiled=True)  13.8 us
    dot_general x1, matrix products, device_step(): jnp.dot(hidden, w_down, preferred_element_type=jnp.float32)  13.2 us
    all_to_all x1, waiting for transfers between devices, device_step(): recv = lax.all_to_all(send, 'data', 0, 0, tiled=True)  10.5 us
    all_to_all x1, starting transfers between devices, device_step(): recv = lax.all_to_all(send, 'data', 0, 0, tiled=True)  6.02 us
  transfers between devices with their start and end apart: 1, of which 1 were waited for; matrix products, arithmetic and copies ran while one was open for 0% of the time, Pallas kernels for 0%

profile of v1, /device:TPU:113, one launch (start us, length us, event | category | flops | bytes accessed | tf_op | source)
XLA Modules:
  0.0 122.9 jit_solution(3485785809136511669)
XLA Ops:
  0.0 0.0 copy-start
  0.0 0.8 and_select_fusion.1
  0.8 0.2 convert_reduce_fusion.1
  1.0 0.1 broadcast_in_dim.7
  1.1 2.2 %convolution_convert_fusion = bf16[192,1664]{1,0:T(8,128)(2,1)} fusion(bf16[64,128]{1,0:T(8,128)(2,1)S(1)} %broadcast_in_dim.7, bf16[64,1536]{1,0:T(8,128)(2,1)} %param.11, s32[64]{0:T(128)S(1)} %multiply_add_fusion), kind=kOutput, calls=%fused_computation.27 | convolution fusion | flops 41652224 | bytes 852224 | tf_op jit(solution)/shard_map/tm,td->md/dot_general | solution.py:28
  3.3 6.0 %all-to-all-start = ((bf16[8,24,1664]{2,1,0:T(8,128)(2,1)}), bf16[8,24,1664]{2,1,0:T(8,128)(2,1)}, u32[]{:S(2)}, u32[]{:S(2)}) async-start(bf16[8,24,1664]{2,1,0:T(8,128)(2,1)} %bitcast.64), calls=%async_computation | async-start | bytes 1277952 | tf_op jit(solution)/shard_map/all_to_all | solution.py:29
  9.3 10.5 %all-to-all-done = bf16[8,24,1664]{2,1,0:T(8,128)(2,1)} async-done(((bf16[8,24,1664]{2,1,0:T(8,128)(2,1)}), bf16[8,24,1664]{2,1,0:T(8,128)(2,1)}, u32[]{:S(2)}, u32[]{:S(2)}) %all-to-all-start) | async-done | bytes 639008 | tf_op jit(solution)/shard_map/all_to_all | solution.py:29
  19.8 0.9 convert_reduce_fusion
  20.7 0.0 copy-done
  20.7 11.8 %fusion.16 = f32[192,8960]{1,0:T(8,128)} fusion(bf16[128,8,8960]{2,1,0:T(8,128)(2,1)} %param.19, bf16[128,8,1536]{2,1,0:T(8,128)(2,1)S(1)} %copy-done, s32[1024]{0:T(1024)S(1)} %add_select_fusion, s32[192]{0:T(256)S(1)} %convert_reduce_fusion, bf16[192,1664]{1,0:T(8,128)(2,1)} %bitcast.1), kind=kOutput, calls=%fused_computation.12 | convolution fusion | flops 4132945920 | bytes 28971776 | tf_op jit(solution)/shard_map/dot_general | solution.py:37
  32.5 12.5 %fusion.22 = f32[192,8960]{1,0:T(8,128)} fusion(bf16[128,8,8960]{2,1,0:T(8,128)(2,1)} %param.17, bf16[128,8,1536]{2,1,0:T(8,128)(2,1)} %param.16, s32[1024]{0:T(1024)S(1)} %add_select_fusion, s32[192]{0:T(256)S(1)} %convert_reduce_fusion, bf16[192,1664]{1,0:T(8,128)(2,1)} %bitcast.1), kind=kOutput, calls=%fused_computation.14 | convolution fusion | flops 4132945920 | bytes 28971776 | tf_op jit(solution)/shard_map/dot_general | solution.py:37
  45.1 16.9 %convolution_add_fusion.1 = f32[192,8960]{1,0:T(8,128)} fusion(f32[192,8960]{1,0:T(8,128)} %fusion.22, bf16[1536,8960]{1,0:T(8,128)(2,1)} %param.13, bf16[192,1664]{1,0:T(8,128)(2,1)} %bitcast.1), kind=kOutput, calls=%fused_computation.10 | convolution fusion | flops 5286543360 | bytes 41877504 | tf_op jit(solution)/shard_map/dot_general | solution.py:40
  61.9 0.0 copy-start.2
  61.9 18.0 %fusion.25 = bf16[192,8960]{1,0:T(8,128)(2,1)} fusion(f32[192,8960]{1,0:T(8,128)} %fusion.16, bf16[1536,8960]{1,0:T(8,128)(2,1)} %param.14, f32[192,8960]{1,0:T(8,128)} %convolution_add_fusion.1, bf16[192,1664]{1,0:T(8,128)(2,1)} %bitcast.1), kind=kOutput, calls=%fused_computation.15 | convolution fusion | flops 5296865280 | bytes 45318144 | tf_op jit(solution)/shard_map/dot_general | solution.py:41
  79.9 0.0 copy-done.2
  79.9 15.0 %fusion.39 = f32[192,1536]{1,0:T(8,128)} fusion(bf16[128,8,1536]{2,1,0:T(8,128)(2,1)S(1)} %copy-done.2, bf16[192,8960]{1,0:T(8,128)(2,1)} %fusion.25, bf16[128,8,8960]{2,1,0:T(8,128)(2,1)} %param.20, s32[1024]{0:T(1024)S(1)} %add_select_fusion, s32[192]{0:T(256)S(1)} %convert_reduce_fusion), kind=kOutput, calls=%fused_computation.26 | convolution fusion | flops 4128669696 | bytes 26120960 | tf_op jit(solution)/shard_map/dot_general | solution.py:37
  94.9 0.0 copy-start.1
  94.9 13.2 %fusion.42 = bf16[192,1536]{1,0:T(8,128)(2,1)S(1)} fusion(f32[192,1536]{1,0:T(8,128)} %fusion.39, bf16[192,8960]{1,0:T(8,128)(2,1)} %fusion.25, bf16[8960,1536]{1,0:T(8,128)(2,1)} %param.15, bf16[192,1664]{1,0:T(8,128)(2,1)} %bitcast.1), kind=kOutput, calls=%fused_computation.28 | convolution fusion | flops 5286002688 | bytes 33325056 | tf_op jit(solution)/shard_map/dot_general | solution.py:43
  108.1 13.8 %all_to_all.24 = bf16[8,24,1536]{2,1,0:T(8,128)(2,1)S(1)} all-to-all(bf16[8,24,1536]{2,1,0:T(8,128)(2,1)S(1)} %bitcast.66), channel_id=1, replica_groups=mesh['rep'=2,'data'=8] {'data'}, dimensions={0} | all-to-all | bytes 1179648 | tf_op jit(solution)/shard_map/all_to_all | solution.py:45
  121.9 0.9 convolution_convert_fusion.1
  122.9 0.0 copy-done.1
  (2 shorter events, 0.0 us)
Async XLA Ops:
  0.0 20.7 %copy-start = (bf16[128,8,1536]{2,1,0:T(8,128)(2,1)S(1)}, bf16[128,8,1536]{2,1,0:T(8,128)(2,1)}, u32[]{:S(2)}) copy-start(bf16[128,8,1536]{2,1,0:T(8,128)(2,1)} %param.18) | copy-start | bytes 9437188
  3.3 16.5 %all-to-all-start = ((bf16[8,24,1664]{2,1,0:T(8,128)(2,1)}), bf16[8,24,1664]{2,1,0:T(8,128)(2,1)}, u32[]{:S(2)}, u32[]{:S(2)}) async-start(bf16[8,24,1664]{2,1,0:T(8,128)(2,1)} %bitcast.64), calls=%async_computation | async-start | bytes 1277952 | tf_op jit(solution)/shard_map/all_to_all | solution.py:29
  61.9 18.0 %copy-start.2 = (bf16[128,8,1536]{2,1,0:T(8,128)(2,1)S(1)}, bf16[128,8,1536]{2,1,0:T(8,128)(2,1)}, u32[]{:S(2)}) copy-start(bf16[128,8,1536]{2,1,0:T(8,128)(2,1)} %param.21) | copy-start | bytes 9437188
  94.9 28.0 %copy-start.1 = (bf16[128,8,1536]{2,1,0:T(8,128)(2,1)S(1)}, bf16[128,8,1536]{2,1,0:T(8,128)(2,1)}, u32[]{:S(2)}) copy-start(bf16[128,8,1536]{2,1,0:T(8,128)(2,1)} %param.18) | copy-start | bytes 9437188

commit v2 on v1

v2 whole, which is shorter than its diff:
```python
import functools

import jax
import jax.numpy as jnp
from jax import lax
from jax.experimental import pallas as pl
from jax.experimental.pallas import tpu as pltpu
from jax.sharding import PartitionSpec as P

ALPHA = 32
ID_LANES = 128
SUB = 256
STEP_SUBS = 5
BF = jnp.bfloat16
F32 = jnp.float32


def nn(a, b):
    return jnp.dot(a, b, preferred_element_type=F32)


def nt(a, b):
    return lax.dot_general(a, b, (((1,), (1,)), ((), ())), preferred_element_type=F32)


def count_ge(v, width, groups):
    total = jnp.zeros(v.shape, jnp.int32)
    for g in range(1, groups):
        total += (v >= g * width).astype(jnp.int32)
    return total


def layer_kernel(groups, rank, cap, per_owner, x_ref, ids_ref, wg, wu, wd, ag, au, bg, bu, ad, bd, out_ref,
                 send, recv, rows, low_g, low_u, hid, low_d, ret, got, a_buf, b_buf, big,
                 ring_sem, a_sem, b_sem, wd_sem, out_sem, in_sem, rs_sem, rr_sem):
    toks, width = x_ref.shape
    ff = wg.shape[1]
    ranks = per_owner * rank
    slots = groups * cap
    scale = ALPHA / rank
    step = STEP_SUBS * SUB
    n_steps = ff // step
    ring_rows = 2 * width + 3 * ranks
    fold = ff // STEP_SUBS
    cols = width // SUB
    parts = ((wg, 0, width), (wu, width, width), (bg, 2 * width, ranks), (bu, 2 * width + ranks, ranks), (ad, 2 * width + 2 * ranks, ranks))
    me = lax.axis_index("data")
    peers = [lax.rem(me + k, groups) for k in (4, 3, 5, 2, 6, 1, 7) if k < groups]

    def ring_copy(c, i):
        src, off, n = parts[i]
        slot = lax.rem(c, 2)
        start = pl.multiple_of(slot * ring_rows + off, 8)
        col = pl.multiple_of(c * step, 128)
        return pltpu.make_async_copy(src.at[:, pl.ds(col, step)], big.at[pl.ds(start, n), :], ring_sem.at[slot, i])

    def wd_at(j):
        return pl.multiple_of(2 * ring_rows + (1 - j) * fold, 8)

    def wd_copy(j, q):
        col = pl.multiple_of(j * SUB, 128)
        return pltpu.make_async_copy(wd.at[pl.ds(q * fold, fold), pl.ds(col, SUB)], big.at[pl.ds(wd_at(j), fold), pl.ds(q * SUB, SUB)], wd_sem.at[j, q])

    def start_wd(j):
        for q in range(STEP_SUBS):
            wd_copy(j, q).start()

    a_copies = [pltpu.make_async_copy(src, a_buf.at[i], a_sem.at[i]) for i, src in enumerate((ag, au))]
    b_copy = pltpu.make_async_copy(bd, b_buf, b_sem)
    for cp in a_copies:
        cp.start()
    for c in range(2):
        for i in range(len(parts)):
            ring_copy(c, i).start()

    barrier = pltpu.get_barrier_semaphore()
    for p in peers:
        pl.semaphore_signal(barrier, inc=1, device_id={"data": p}, device_id_type=pl.DeviceIdType.MESH)

    id_row = ids_ref[...]
    sub_i = lax.broadcasted_iota(jnp.int32, (toks, toks), 0)
    lane_i = lax.broadcasted_iota(jnp.int32, (toks, toks), 1)
    id_col = jnp.sum(jnp.where(sub_i == lane_i, jnp.broadcast_to(id_row, (toks, toks)), 0), axis=1, keepdims=True)
    own_row = count_ge(id_row, per_owner, groups)
    own_col = count_ge(id_col, per_owner, groups)
    same = own_col == own_row
    arr_col = jnp.sum((same & (lane_i < sub_i)).astype(jnp.int32), axis=1, keepdims=True)
    arr_row = jnp.sum((same & (sub_i < lane_i)).astype(jnp.int32), axis=0, keepdims=True)
    to_slot = (lax.broadcasted_iota(jnp.int32, (slots, toks), 0) == own_row * cap + arr_row).astype(F32).astype(BF)
    local = (id_col - own_col * per_owner).astype(F32).astype(BF)
    payload = jnp.concatenate([x_ref[...], jnp.broadcast_to(local, (toks, ID_LANES))], axis=1)
    send[...] = nn(to_slot, payload).reshape(groups, cap, width + ID_LANES).astype(BF)

    pl.semaphore_wait(barrier, groups - 1)

    def row_copy(p):
        return pltpu.make_async_remote_copy(src_ref=send.at[p], dst_ref=recv.at[me], send_sem=out_sem.at[p], recv_sem=in_sem.at[me],
                                            device_id={"data": p}, device_id_type=pl.DeviceIdType.MESH)

    def row_arrival(p):
        return pltpu.make_async_remote_copy(src_ref=send.at[p], dst_ref=recv.at[p], send_sem=out_sem.at[p], recv_sem=in_sem.at[p],
                                            device_id={"data": p}, device_id_type=pl.DeviceIdType.MESH)

    for p in peers:
        row_copy(p).start()
    recv[me] = send[me]
    for p in peers:
        row_arrival(p).wait_recv()

    b_copy.start()
    start_wd(0)
    start_wd(1)

    landed = recv[...].astype(F32).reshape(slots, width + ID_LANES)
    rows[...] = landed[:, :width].astype(BF)
    first = landed[:, width:width + 1].astype(jnp.int32) * rank
    rank_i = lax.broadcasted_iota(jnp.int32, (slots, ranks), 1)
    own = (rank_i >= first) & (rank_i < first + rank)
    for i, low in enumerate((low_g, low_u)):
        a_copies[i].wait()
        low[...] = jnp.where(own, nt(rows[...], a_buf[i]), 0.0).astype(BF)
    low_d[...] = jnp.zeros_like(low_d)

    def half(base, col, w_off, w_n, b_off, low):
        full = nn(low[...], big[pl.ds(base + b_off, ranks), col])
        return nn(rows[...], big[pl.ds(base + w_off, w_n), col]) + (scale * full).astype(BF).astype(F32)

    def ff_step(c, carry):
        for i in range(len(parts)):
            ring_copy(c, i).wait()
        base = pl.multiple_of(lax.rem(c, 2) * ring_rows, 8)
        for s in range(STEP_SUBS):
            col = pl.ds(s * SUB, SUB)
            g = half(base, col, 0, width, 2 * width, low_g)
            u = half(base, col, width, width, 2 * width + ranks, low_u)
            hid[c * STEP_SUBS + s] = (g * jax.nn.sigmoid(g) * u).astype(BF)
        h = jnp.concatenate([hid[c * STEP_SUBS + s] for s in range(STEP_SUBS)], axis=1)
        low_d[...] += nt(h, big[pl.ds(base + 2 * width + 2 * ranks, ranks), :])

        @pl.when(c + 2 < n_steps)
        def _():
            for i in range(len(parts)):
                ring_copy(c + 2, i).start()

        @pl.when(c == n_steps - 2)
        def _():
            for j in range(2, 5):
                start_wd(j)

        return carry

    lax.fori_loop(0, n_steps, ff_step, 0)
    start_wd(5)

    low_dm = jnp.where(own, low_d[...], 0.0).astype(BF)
    low_g[...] = low_dm
    b_copy.wait()

    def back_copy(j, p):
        return pltpu.make_async_remote_copy(src_ref=ret.at[j, p], dst_ref=got.at[j, me], send_sem=rs_sem.at[j, p], recv_sem=rr_sem.at[j, me],
                                            device_id={"data": p}, device_id_type=pl.DeviceIdType.MESH)

    def back_arrival(j, p):
        return pltpu.make_async_remote_copy(src_ref=ret.at[j, p], dst_ref=got.at[j, p], send_sem=rs_sem.at[j, p], recv_sem=rr_sem.at[j, p],
                                            device_id={"data": p}, device_id_type=pl.DeviceIdType.MESH)

    def col_step(j, carry):
        for q in range(STEP_SUBS):
            wd_copy(j, q).wait()
        col = pl.ds(pl.multiple_of(j * SUB, 128), SUB)
        full = nn(low_g[...], b_buf[:, col])
        per = fold // SUB
        acc = jnp.zeros((slots, SUB), F32)
        for q in range(STEP_SUBS):
            h = jnp.concatenate([hid[q * per + s] for s in range(per)], axis=1)
            acc += nn(h, big[pl.ds(wd_at(j), fold), pl.ds(q * SUB, SUB)])
        done = rows[:, col].astype(F32) + (acc + (scale * full).astype(BF).astype(F32))
        ret[j] = done.reshape(groups, cap, SUB).astype(BF)
        for p in peers:
            back_copy(j, p).start()
        got[j, me] = ret[j, me]
        return carry

    lax.fori_loop(0, cols, col_step, 0)

    to_tok = (lax.broadcasted_iota(jnp.int32, (toks, slots), 1) == own_col * cap + arr_col).astype(F32).astype(BF)
    for j in range(cols):
        for p in peers:
            back_arrival(j, p).wait_recv()
        block = got[j].astype(F32).reshape(slots, SUB).astype(BF)
        out_ref[:, j * SUB:(j + 1) * SUB] = nn(to_tok, block).astype(BF)
    for p in peers:
        row_copy(p).wait_send()
        for j in range(cols):
            back_copy(j, p).wait_send()


def solution(mesh):
    groups = mesh.shape["data"]
    row_spec = P(("rep", "data"), None)
    id_spec = P(("rep", "data"))
    owned_spec = P("data", None, None)

    def device_step(x, adapter_id, w_gate, w_up, w_down, a_gate, b_gate, a_up, b_up, a_down, b_down):
        toks, width = x.shape
        per_owner, rank, ff = b_gate.shape
        ranks = per_owner * rank
        cap = (3 * toks + groups - 1) // groups
        slots = groups * cap
        cols = width // SUB
        ring_rows = 2 * width + 3 * ranks
        fold = ff // STEP_SUBS

        def flat(m):
            return m.reshape(ranks, m.shape[-1])

        return pl.pallas_call(
            functools.partial(layer_kernel, groups, rank, cap, per_owner),
            out_shape=jax.ShapeDtypeStruct((toks, width), BF),
            in_specs=[pl.BlockSpec(memory_space=pltpu.VMEM)] * 2 + [pl.BlockSpec(memory_space=pl.ANY)] * 9,
            out_specs=pl.BlockSpec(memory_space=pltpu.VMEM),
            scratch_shapes=[
                pltpu.VMEM((groups, cap, width + ID_LANES), BF),
                pltpu.VMEM((groups, cap, width + ID_LANES), BF),
                pltpu.VMEM((slots, width), BF),
                pltpu.VMEM((slots, ranks), BF),
                pltpu.VMEM((slots, ranks), BF),
                pltpu.VMEM((ff // SUB, slots, SUB), BF),
                pltpu.VMEM((slots, ranks), F32),
                pltpu.VMEM((cols, groups, cap, SUB), BF),
                pltpu.VMEM((cols, groups, cap, SUB), BF),
                pltpu.VMEM((2, ranks, width), BF),
                pltpu.VMEM((ranks, width), BF),
                pltpu.VMEM((2 * ring_rows + 2 * fold, STEP_SUBS * SUB), BF),
                pltpu.SemaphoreType.DMA((2, 5)),
                pltpu.SemaphoreType.DMA((2,)),
                pltpu.SemaphoreType.DMA,
                pltpu.SemaphoreType.DMA((cols, STEP_SUBS)),
                pltpu.SemaphoreType.DMA((groups,)),
                pltpu.SemaphoreType.DMA((groups,)),
                pltpu.SemaphoreType.DMA((cols, groups)),
                pltpu.SemaphoreType.DMA((cols, groups)),
            ],
            compiler_params=pltpu.CompilerParams(collective_id=0, has_side_effects=True, vmem_limit_bytes=67_000_000),
            name="lora_layer",
        )(x, adapter_id.reshape(1, toks), w_gate, w_up, w_down, flat(a_gate), flat(a_up), flat(b_gate), flat(b_up), flat(a_down), flat(b_down))

    return jax.shard_map(device_step, mesh=mesh, in_specs=(row_spec, id_spec, P(), P(), P(), owned_spec, owned_spec, owned_spec, owned_spec, owned_spec, owned_spec), out_specs=row_spec, check_vma=False)
```

time: 123 us -> 62.7 us (0.51)
  matrix products: 90.5 us -> 0 us
  Pallas kernels: 0 us -> 61 us
  blocking collectives: 13.8 us -> 0 us
  waiting for transfers between devices: 10.5 us -> 0 us
  starting transfers between devices: 6.02 us -> 0 us
  other arithmetic: 1.91 us -> 0 us
  local copies, waits for them, and re-layouts: 0.09 us -> 1.62 us
    dot_general x8 -> x0, matrix products: 90.5 us -> none  [the longest x3 39.3 us: delta(): jnp.dot(low, b_mat.reshape(per_owner * rank, -1), preferred_element_type=...]
    pallas_call x0 -> x1, Pallas kernels: none -> 61 us  [device_step(): pl.pallas_call(functools.partial(layer_kernel, groups, rank, cap, per_own...]
    all_to_all x1 -> x0, blocking collectives: 13.8 us -> none  [device_step(): back = lax.all_to_all(done, 'data', 0, 0, tiled=True)]
    all_to_all x1 -> x0, waiting for transfers between devices: 10.5 us -> none  [device_step(): recv = lax.all_to_all(send, 'data', 0, 0, tiled=True)]
    all_to_all x1 -> x0, starting transfers between devices: 6.02 us -> none  [device_step(): recv = lax.all_to_all(send, 'data', 0, 0, tiled=True)]
    unnamed x6 -> x1, local copies, waits for them, and re-layouts: 0.01 us -> 1.62 us
  transfers between devices with their start and end apart: 1 -> 0, of which waited for: 1 -> 0; matrix products, arithmetic and copies ran while one was open for 0% -> 0% of each run, Pallas kernels for 0% -> 0%
where the time goes in v2:
time: 62.7 us; the launch traced here: 62.6 us
  Pallas kernels  61 us (97%)
  local copies, waits for them, and re-layouts  1.62 us (3%)
    pallas_call x1, Pallas kernels, device_step(): pl.pallas_call(functools.partial(layer_kernel, groups, rank, cap, per_own...  61 us
    unnamed x1, local copies, waits for them, and re-layouts  1.62 us

profile of v2, /device:TPU:113, one launch (start us, length us, event | category | flops | bytes accessed | tf_op | source)
XLA Modules:
  0.0 62.6 jit_solution(17171484798874790810)
XLA Ops:
  0.0 61.0 %lora_layer.1 = bf16[64,1536]{1,0:T(8,128)(2,1)} custom-call(bf16[64,1536]{1,0:T(8,128)(2,1)} %x_ref.1, s32[1,64]{1,0:T(1,128)} %bitcast.13, bf16[1536,8960]{1,0:T(8,128)(2,1)} %wg.1, bf16[1536,8960]{1,0:T(8,128)(2,1)} %wu.1, bf16[8960,1536]{1,0:T(8,128)(2,1)} %wd.1, bf16[1024,1536]{1,0:T(8,128)(2,1)} %bitcast.10, bf16[1024,1536]{1,0:T(8,128)(2,1)} %bitcast.11, ...), custom_call_target="tpu_custom_call" | custom-call | tf_op jit(solution)/shard_map/lora_layer/pallas_call | solution.py:217
  61.0 1.6 %copy.13 = bf16[64,1536]{1,0:T(8,128)(2,1)} copy(bf16[64,1536]{1,0:T(8,128)(2,1)} %lora_layer.1) | data formatting | bytes 393216
